TPU v7x, 32 devices: a whole 2x2x4 slice. The times are simulated.
32 devices in a mesh: dp: 16 (over z, y, x), mp: 2 (over core).
Axes of the slice: x: 2, y: 2, z: 4, core: 2. Of those that a mesh axis runs over, the one named last changes fastest.
Arguments:
- hidden_state: bfloat16 [32, 19, 19, 256], P('dp'), may hold values from -6 to 6
- actions: int32 [32, 2], P('dp'), may hold values from 0 to 361
- value_target: int32 [32, 2], P('dp'), may hold values from 0 to 600
- reward_target: int32 [32, 2], P('dp'), may hold values from 0 to 600
- kernel_first: float32 [3, 3, 256, 256], P(None, None, 'dp', 'mp'), may hold values from -6 to 6
- kernel_second: float32 [3, 3, 256, 256], P(None, None, 'dp', 'mp'), may hold values from -6 to 6
- head_weight: float32 [2, 256, 601], P('mp', 'dp'), may hold values from -6 to 6
- action_embed: float32 [2, 256], P('mp', 'dp'), may hold values from -6 to 6
- first_mean: float32 [3, 3, 256, 256], P(None, None, 'dp', 'mp'), may hold values from -0.00061035156 to 0.00061035156
- first_square: float32 [3, 3, 256, 256], P(None, None, 'dp', 'mp'), may hold values from 1e-09 to 1e-06
- second_mean: float32 [3, 3, 256, 256], P(None, None, 'dp', 'mp'), may hold values from -0.00061035156 to 0.00061035156
- second_square: float32 [3, 3, 256, 256], P(None, None, 'dp', 'mp'), may hold values from 1e-09 to 1e-06
- head_mean: float32 [2, 256, 601], P('mp', 'dp'), may hold values from -0.0029296875 to 0.0029296875
- head_square: float32 [2, 256, 601], P('mp', 'dp'), may hold values from 1e-08 to 1e-06
- embed_mean: float32 [2, 256], P('mp', 'dp'), may hold values from -0.0017089844 to 0.0017089844
- embed_square: float32 [2, 256], P('mp', 'dp'), may hold values from 1e-09 to 1e-06
Outputs:
- kernel_first_new: float32 [3, 3, 256, 256], P(None, None, 'dp', 'mp')
- kernel_second_new: float32 [3, 3, 256, 256], P(None, None, 'dp', 'mp')
- head_weight_new: float32 [2, 256, 601], P('mp', 'dp')
- action_embed_new: float32 [2, 256], P('mp', 'dp')
- first_mean_new: float32 [3, 3, 256, 256], P(None, None, 'dp', 'mp')
- first_square_new: float32 [3, 3, 256, 256], P(None, None, 'dp', 'mp')
- second_mean_new: float32 [3, 3, 256, 256], P(None, None, 'dp', 'mp')
- second_square_new: float32 [3, 3, 256, 256], P(None, None, 'dp', 'mp')
- head_mean_new: float32 [2, 256, 601], P('mp', 'dp')
- head_square_new: float32 [2, 256, 601], P('mp', 'dp')
- embed_mean_new: float32 [2, 256], P('mp', 'dp')
- embed_square_new: float32 [2, 256], P('mp', 'dp')
- first_grad: float32 [3, 3, 256, 256], P(None, None, 'dp', 'mp')
- second_grad: float32 [3, 3, 256, 256], P(None, None, 'dp', 'mp')
- head_grad: float32 [2, 256, 601], P('mp', 'dp')
- embed_grad: float32 [2, 256], P('mp', 'dp')
Inputs may be any that keep to these rules, and one draw needn't show every extreme that they name: `actions`: the value 361 stands for a pass.
All inputs are finite; a program needn't handle non-finite values.
Results may differ from a plain program's by a relative error of at most 0.02.
Values may be sent and summed in bfloat16 or wider, within the bound.
A program may use at most 64 MiB of HBM per device.

v0:
```python
import jax
import jax.numpy as jnp
from jax import lax
from jax.sharding import PartitionSpec as P

CHANNELS = 256


head_scale = 4.0
soft_cap = 15.0
eps_norm = 1e-05
beta_one = 0.9
beta_two = 0.999
step_size = 0.1
eps_adam = 1e-08


def conv_apply(field, kernel, layout):
    return lax.conv_general_dilated(
        field,
        kernel,
        (1, 1),
        "SAME",
        dimension_numbers=("NHWC", layout, "NHWC"),
        preferred_element_type=jnp.float32,
    )


def gate_slope(pre):
    sig = jax.nn.sigmoid(pre)
    return sig * (1.0 + pre * (1.0 - sig))


def tap_products(field, grad, field_rows):
    side = field.shape[1]
    padded = jnp.pad(field, ((0, 0), (1, 1), (1, 1), (0, 0)))
    flat_grad = grad.reshape(-1, grad.shape[3])
    blocks = []
    for offset in range(9):
        row_start = offset // 3
        col_start = offset % 3
        window = padded[:, row_start : row_start + side, col_start : col_start + side, :].reshape(
            -1, field.shape[3]
        )
        if field_rows:
            blocks.append(
                lax.dot_general(
                    window, flat_grad, (((0,), (0,)), ((), ())), preferred_element_type=jnp.float32
                )
            )
        else:
            blocks.append(
                lax.dot_general(
                    flat_grad, window, (((0,), (0,)), ((), ())), preferred_element_type=jnp.float32
                )
            )
    stacked = jnp.stack(blocks)
    return stacked.reshape(3, 3, stacked.shape[1], stacked.shape[2])


def action_planes(move, board):
    cells = board * board
    plane = (lax.broadcasted_iota(jnp.int32, (move.shape[0], cells), 1) == move[:, None]).astype(
        jnp.float32
    )
    passed = (move == cells).astype(jnp.float32)
    return (plane.reshape(move.shape[0], board, board, 1), passed[:, None, None, None])


def head_backward(state, head_used, value_now, reward_now, total):
    pooled = jnp.mean(state, axis=(1, 2)).astype(jnp.bfloat16)
    raw = head_scale * jnp.stack(
        [
            jnp.dot(pooled, head_used[0], preferred_element_type=jnp.float32),
            jnp.dot(pooled, head_used[1], preferred_element_type=jnp.float32),
        ]
    )
    squashed = jnp.tanh(raw / soft_cap)
    raised = jnp.exp(soft_cap * squashed)
    chances = raised / jnp.sum(raised, axis=2, keepdims=True)
    targets = jnp.stack([value_now, reward_now])
    picked = (lax.broadcasted_iota(jnp.int32, raw.shape, 2) == targets[:, :, None]).astype(
        jnp.float32
    )
    logit_grad = ((chances - picked) * (1.0 - squashed * squashed) / total).astype(jnp.bfloat16)
    pooled_grad = head_scale * (
        jnp.dot(logit_grad[0], head_used[0].T, preferred_element_type=jnp.float32)
        + jnp.dot(logit_grad[1], head_used[1].T, preferred_element_type=jnp.float32)
    )
    return (pooled, logit_grad, pooled_grad)


def adam_update(param, grad, mean, square):
    mean_new = beta_one * mean + (1.0 - beta_one) * grad
    square_new = beta_two * square + (1.0 - beta_two) * grad * grad
    param_new = param - step_size * mean_new / (jnp.sqrt(square_new) + eps_adam)
    return (param_new, mean_new, square_new)


def local(
    hidden_state,
    actions,
    value_target,
    reward_target,
    kernel_first,
    kernel_second,
    head_weight,
    action_embed,
    first_mean,
    first_square,
    second_mean,
    second_square,
    head_mean,
    head_square,
    embed_mean,
    embed_square,
):
    total = hidden_state.shape[0] * lax.axis_size("dp")
    board = hidden_state.shape[1]
    cells = board * board
    scale = (9.0 * CHANNELS) ** (-0.5)
    first_used, second_used, head_used, embed_used = (
        lax.all_gather(kernel_first.astype(jnp.bfloat16), "dp", axis=2, tiled=True),
        lax.all_gather(kernel_second.astype(jnp.bfloat16), "dp", axis=2, tiled=True),
        lax.all_gather(head_weight.astype(jnp.bfloat16), "dp", axis=1, tiled=True),
        lax.all_gather(action_embed.astype(jnp.bfloat16), "dp", axis=1, tiled=True),
    )
    first_used, second_used, head_used, embed_used = (
        lax.all_gather(first_used, "mp", axis=3, tiled=True),
        lax.all_gather(second_used, "mp", axis=3, tiled=True),
        lax.all_gather(head_used, "mp", axis=0, tiled=True),
        lax.all_gather(embed_used, "mp", axis=0, tiled=True),
    )
    count = hidden_state.shape[0] // lax.axis_size("mp")
    begin = lax.axis_index("mp") * count
    states = lax.dynamic_slice_in_dim(hidden_state, begin, count, 0)
    moves = lax.dynamic_slice_in_dim(actions, begin, count, 0)
    values = lax.dynamic_slice_in_dim(value_target, begin, count, 0)
    rewards = lax.dynamic_slice_in_dim(reward_target, begin, count, 0)
    unroll = moves.shape[1]
    embed = embed_used.astype(jnp.float32)
    state = states.astype(jnp.float32)
    saved = []
    for position in range(unroll):
        plane, passed = action_planes(moves[:, position], board)
        mixed = state + plane * embed[0] + passed * embed[1]
        conv_input = mixed.astype(jnp.bfloat16)
        pre = scale * conv_apply(conv_input, first_used, "HWIO")
        hidden = jax.nn.silu(pre).astype(jnp.bfloat16)
        branch = conv_apply(hidden, second_used, "HWOI")
        summed = mixed + scale * branch
        factor = lax.rsqrt(jnp.mean(summed * summed, axis=(1, 2, 3), keepdims=True) + eps_norm)
        state = summed * factor
        pooled, logit_grad, pooled_grad = head_backward(
            state, head_used, values[:, position], rewards[:, position], total
        )
        saved.append(
            (
                plane,
                passed,
                conv_input,
                pre,
                hidden,
                summed,
                factor,
                pooled,
                logit_grad,
                pooled_grad,
            )
        )
    first_grad = jnp.zeros(first_used.shape, jnp.float32)
    second_grad = jnp.zeros(second_used.shape, jnp.float32)
    head_grad = jnp.zeros(head_used.shape, jnp.float32)
    embed_grad = jnp.zeros(embed_used.shape, jnp.float32)
    carry = jnp.zeros(states.shape, jnp.float32)
    for position in range(unroll - 1, -1, -1):
        plane, passed, conv_input, pre, hidden, summed, factor, pooled, logit_grad, pooled_grad = (
            saved[position]
        )
        state_grad = carry + pooled_grad[:, None, None, :] / cells
        summed_grad = factor * state_grad - factor * factor * factor * summed * jnp.mean(
            state_grad * summed, axis=(1, 2, 3), keepdims=True
        )
        branch_grad = summed_grad.astype(jnp.bfloat16)
        hidden_grad = scale * conv_apply(branch_grad, second_used[::-1, ::-1], "HWIO")
        inner_grad = (hidden_grad * gate_slope(pre)).astype(jnp.bfloat16)
        input_grad = conv_apply(inner_grad, first_used[::-1, ::-1], "HWOI")
        carry = summed_grad + scale * input_grad
        first_grad = first_grad + scale * tap_products(conv_input, inner_grad, True)
        second_grad = second_grad + scale * tap_products(hidden, branch_grad, False)
        head_grad = head_grad + head_scale * jnp.stack(
            [
                lax.dot_general(
                    pooled,
                    logit_grad[0],
                    (((0,), (0,)), ((), ())),
                    preferred_element_type=jnp.float32,
                ),
                lax.dot_general(
                    pooled,
                    logit_grad[1],
                    (((0,), (0,)), ((), ())),
                    preferred_element_type=jnp.float32,
                ),
            ]
        )
        embed_grad = embed_grad + jnp.stack(
            [jnp.sum(plane * carry, axis=(0, 1, 2)), jnp.sum(passed * carry, axis=(0, 1, 2))]
        )
    first_grad, second_grad, head_grad, embed_grad = (
        lax.psum_scatter(first_grad, "mp", scatter_dimension=3, tiled=True),
        lax.psum_scatter(second_grad, "mp", scatter_dimension=3, tiled=True),
        lax.psum_scatter(head_grad, "mp", scatter_dimension=0, tiled=True),
        lax.psum_scatter(embed_grad, "mp", scatter_dimension=0, tiled=True),
    )
    first_grad, second_grad, head_grad, embed_grad = (
        lax.psum_scatter(first_grad, "dp", scatter_dimension=2, tiled=True),
        lax.psum_scatter(second_grad, "dp", scatter_dimension=2, tiled=True),
        lax.psum_scatter(head_grad, "dp", scatter_dimension=1, tiled=True),
        lax.psum_scatter(embed_grad, "dp", scatter_dimension=1, tiled=True),
    )
    first_new, first_mean_new, first_square_new = adam_update(
        kernel_first, first_grad, first_mean, first_square
    )
    second_new, second_mean_new, second_square_new = adam_update(
        kernel_second, second_grad, second_mean, second_square
    )
    head_new, head_mean_new, head_square_new = adam_update(
        head_weight, head_grad, head_mean, head_square
    )
    embed_new, embed_mean_new, embed_square_new = adam_update(
        action_embed, embed_grad, embed_mean, embed_square
    )
    return (
        first_new,
        second_new,
        head_new,
        embed_new,
        first_mean_new,
        first_square_new,
        second_mean_new,
        second_square_new,
        head_mean_new,
        head_square_new,
        embed_mean_new,
        embed_square_new,
        first_grad,
        second_grad,
        head_grad,
        embed_grad,
    )


def solution(mesh):
    placed = (
        P("dp", None, None, None),
        P("dp", None),
        P("dp", None),
        P("dp", None),
        P(None, None, "dp", "mp"),
        P(None, None, "dp", "mp"),
        P("mp", "dp", None),
        P("mp", "dp"),
        P(None, None, "dp", "mp"),
        P(None, None, "dp", "mp"),
        P(None, None, "dp", "mp"),
        P(None, None, "dp", "mp"),
        P("mp", "dp", None),
        P("mp", "dp", None),
        P("mp", "dp"),
        P("mp", "dp"),
    )
    return jax.shard_map(
        local,
        mesh=mesh,
        in_specs=placed,
        out_specs=(
            P(None, None, "dp", "mp"),
            P(None, None, "dp", "mp"),
            P("mp", "dp", None),
            P("mp", "dp"),
            P(None, None, "dp", "mp"),
            P(None, None, "dp", "mp"),
            P(None, None, "dp", "mp"),
            P(None, None, "dp", "mp"),
            P("mp", "dp", None),
            P("mp", "dp", None),
            P("mp", "dp"),
            P("mp", "dp"),
            P(None, None, "dp", "mp"),
            P(None, None, "dp", "mp"),
            P("mp", "dp", None),
            P("mp", "dp"),
        ),
        check_vma=False,
    )
```

profile of v0, /device:TPU:0, one launch (start us, length us, event | category | flops | bytes accessed | tf_op | source)
XLA Modules:
  0.0 581.1 jit_solution(16968905555778703401)
XLA Ops:
  7.3 1.0 convert_element_type.150
  8.3 48.3 %all_gather.26 = bf16[3,3,256,128]{3,2,1,0:T(8,128)(2,1)} all-gather(bf16[3,3,16,128]{3,2,1,0:T(8,128)(2,1)S(1)} %convert_element_type.150), channel_id=1, replica_groups=mesh['dp'=16,'mp'=2] {'dp'}, dimensions={2}, use_global_device_ids=true | all-gather | bytes 626688 | tf_op jit(solution)/shard_map/all_gather | solution.py:123
  56.6 0.9 convert_element_type.152
  57.5 41.0 %all_gather.28 = bf16[3,3,256,128]{3,2,1,0:T(8,128)(2,1)} all-gather(bf16[3,3,16,128]{3,2,1,0:T(8,128)(2,1)S(1)} %convert_element_type.152), channel_id=1, replica_groups=mesh['dp'=16,'mp'=2] {'dp'}, dimensions={2}, use_global_device_ids=true | all-gather | bytes 626688 | tf_op jit(solution)/shard_map/all_gather | solution.py:124
  100.1 38.8 %all-reduce.4 = bf16[256]{0:T(256)(128)(2,1)S(1)} all-reduce(bf16[256]{0:T(256)(128)(2,1)S(1)} %dynamic-update-slice), channel_id=1, replica_groups=mesh['dp'=16,'mp'=2] {'dp'}, use_global_device_ids=true, to_apply=%add.4 | all-reduce | flops 256 | bytes 1024
  138.9 1.8 all-gather
  144.4 37.2 %all_gather.30 = bf16[1,256,601]{2,1,0:T(8,128)(2,1)S(1)} all-gather(bf16[1,16,601]{2,1,0:T(8,128)(2,1)S(1)} %convert_element_type.157), channel_id=1, replica_groups=mesh['dp'=16,'mp'=2] {'dp'}, dimensions={1}, use_global_device_ids=true | all-gather | bytes 326944 | tf_op jit(solution)/shard_map/all_gather | solution.py:125
  183.4 1.4 add_reduce_fusion
  184.8 1.4 add_reduce_fusion.1
  186.2 2.4 all_gather.31
  188.6 0.8 fusion.61
  189.5 2.0 fusion.6
  192.3 2.0 convolution_multiply_fusion.3
  194.8 0.8 multiply_reduce_fusion.8
  197.4 2.1 fusion.5
  199.5 0.8 select_bitcast_fusion.2
  201.7 0.8 multiply_reduce_fusion.7
  207.8 2.1 fusion.7
  211.9 0.8 multiply_reduce_fusion.3
  213.3 0.8 fusion.348
  214.2 1.0 pad.29
  216.4 1.2 fusion
  218.3 1.2 fusion.17
  219.6 1.2 fusion.16
  220.8 1.3 fusion.15
  222.1 1.2 fusion.14
  223.4 1.2 fusion.13
  224.6 1.2 fusion.12
  225.9 1.2 fusion.11
  227.1 1.3 fusion.10
  228.4 1.2 fusion.9
  229.8 0.9 reshape.830
  230.6 1.0 slice_bitcast_fusion.9
  231.6 1.2 fusion.26
  235.6 2.0 add_multiply_fusion
  237.7 0.8 copy-done.8
  238.7 2.0 fusion.8
  247.1 1.7 add_multiply_fusion.1
  251.8 2.5 all-reduce.5
  254.9 0.8 copy.106
  257.3 1.5 reduce-scatter.10.cloned.1.call-done
  258.8 80.4 %reduce-scatter.22.cloned.1.call-done = f32[16,1]{1,0:T(8,128)} async-done(((f32[256,1]{1,0:T(8,128)}), f32[16,1]{1,0:T(8,128)}) %reduce-scatter.22.cloned.1.call-update) | async-done | bytes 80
  340.5 75.6 %reduce-scatter.20.cloned.1.call-done = f32[1,16,601]{2,1,0:T(8,128)} async-done(((f32[1,256,601]{2,1,0:T(8,128)}), f32[1,16,601]{2,1,0:T(8,128)}) %reduce-scatter.20.cloned.1.call-update) | async-done | bytes 38480 | tf_op jit(solution)/shard_map/reduce_scatter | solution.py:219
  416.1 1.4 divide_subtract_fusion.2
  417.6 77.1 %reduce-scatter.16.cloned.1.call-done = f32[3,3,16,128]{3,2,1,0:T(8,128)} async-done(((f32[3,3,256,128]{3,2,1,0:T(8,128)}), f32[3,3,16,128]{3,2,1,0:T(8,128)}) %reduce-scatter.16.cloned.1.call-update) | async-done | bytes 73744 | tf_op jit(solution)/shard_map/reduce_scatter | solution.py:218
  494.6 1.6 divide_subtract_fusion
  496.2 76.8 %reduce-scatter.12.cloned.1.call-done = f32[3,3,16,128]{3,2,1,0:T(8,128)} async-done(((f32[3,3,256,128]{3,2,1,0:T(8,128)}), f32[3,3,16,128]{3,2,1,0:T(8,128)}) %reduce-scatter.12.cloned.1.call-update) | async-done | bytes 73744 | tf_op jit(solution)/shard_map/reduce_scatter | solution.py:217
  573.0 1.6 divide_subtract_fusion.1
  (222 shorter events, 31.9 us)
Async XLA Ops:
  7.2 136.1 %copy-start = (bf16[2,19,19,256]{3,0,2,1:T(2,128)(2,1)S(1)}, bf16[2,19,19,256]{3,0,2,1:T(2,128)(2,1)}, u32[]{:S(2)}) copy-start(bf16[2,19,19,256]{3,0,2,1:T(2,128)(2,1)} %param.16) | copy-start | bytes 1108996
  7.2 91.4 %copy-start.38 = (u32[32]{0:T(128)S(1)}, u32[32]{0:T(128)}, u32[]{:S(2)}) copy-start(u32[32]{0:T(128)} %constant.145) | copy-start | bytes 388
  7.2 91.4 %copy-start.28 = (f32[1,16]{1,0:T(1,128)S(1)}, f32[1,16]{1,0:T(1,128)}, u32[]{:S(2)}) copy-start(f32[1,16]{1,0:T(1,128)} %param.23) | copy-start | bytes 196
  7.2 133.5 %copy-start.36 = (s32[2,2]{1,0:T(2,128)S(1)}, s32[2,2]{1,0:T(2,128)}, u32[]{:S(2)}) copy-start(s32[2,2]{1,0:T(2,128)} %param.17) | copy-start | bytes 52
  7.2 137.1 %copy-start.17 = (f32[1,16,601]{2,1,0:T(8,128)S(1)}, f32[1,16,601]{2,1,0:T(8,128)}, u32[]{:S(2)}) copy-start(f32[1,16,601]{2,1,0:T(8,128)} %param.22) | copy-start | bytes 115396
  7.2 174.4 %copy-start.32 = (s32[2,2]{1,0:T(2,128)S(1)}, s32[2,2]{1,0:T(2,128)}, u32[]{:S(2)}) copy-start(s32[2,2]{1,0:T(2,128)} %param.18) | copy-start | bytes 52
  7.3 174.4 %copy-start.31 = (s32[2,2]{1,0:T(2,128)S(1)}, s32[2,2]{1,0:T(2,128)}, u32[]{:S(2)}) copy-start(s32[2,2]{1,0:T(2,128)} %param.19) | copy-start | bytes 52
  7.3 182.2 %all-gather.4.cloned.1.call-start = ((), (), s32[]{:S(2)}) async-start(), calls=%async_computation.7 | async-start | bytes 1769472 | tf_op jit(solution)/shard_map/all_gather | solution.py:129
  56.6 135.1 %all-gather.6.cloned.1.call-start = ((), (), s32[]{:S(2)}) async-start(), calls=%async_computation.8 | async-start | bytes 1769472 | tf_op jit(solution)/shard_map/all_gather | solution.py:130
  98.5 157.2 %reduce-scatter.18.cloned.1.call-start = ((), (), s32[]{:S(2)}) async-start(), calls=%async_computation.13 | async-start | bytes 1966080 | tf_op jit(solution)/shard_map/reduce_scatter | solution.py:213
  181.6 7.9 %copy-start.26 = (pred[8,3]{0,1:T(4,128)(4,1)S(1)}, pred[8,3]{0,1:T(4,128)(4,1)}, u32[]{:S(2)}) copy-start(pred[8,3]{0,1:T(4,128)(4,1)} %constant.135) | copy-start | bytes 76
  191.5 0.8 copy-start.9
  196.4 0.7 copy-start.1
  197.4 3.0 copy-start.35
  199.5 0.9 copy-start.11
  204.5 3.3 copy-start.12
  207.8 2.8 copy-start.33
  209.9 0.7 copy-start.5
  215.3 2.3 copy-start.7
  217.7 38.8 %reduce-scatter.14.cloned.1.call-start = ((), (), s32[]{:S(2)}) async-start(), calls=%async_computation.11 | async-start | bytes 3538944 | tf_op jit(solution)/shard_map/reduce_scatter | solution.py:212
  227.1 2.5 copy-start.3
  230.6 2.2 copy-start.16
  233.2 0.9 copy-start.4
  237.6 0.9 copy-start.8
  237.6 1.1 copy-start.10
  237.6 1.2 copy-start.19
  237.6 3.1 copy-start.6
  237.6 3.8 copy-start.15
  237.6 21.2 %reduce-scatter.10.cloned.1.call-start = ((), (), s32[]{:S(2)}) async-start(), calls=%async_computation.9 | async-start | bytes 3538944 | tf_op jit(solution)/shard_map/reduce_scatter | solution.py:211
  243.5 1.0 copy-start.2
  248.8 0.7 copy-start.37
  248.8 1.4 copy-start.34
  248.9 90.3 %reduce-scatter.22.cloned.1.call-start = ((), (), s32[]{:S(2)}) async-start(), calls=%async_computation.15 | async-start | bytes 139264
  251.5 88.5 %copy-start.29 = (f32[1,16]{1,0:T(1,128)S(1)}, f32[1,16]{1,0:T(1,128)}, u32[]{:S(2)}) copy-start(f32[1,16]{1,0:T(1,128)} %param.30) | copy-start | bytes 196
  251.5 88.5 %copy-start.30 = (f32[1,16]{1,0:T(1,128)S(1)}, f32[1,16]{1,0:T(1,128)}, u32[]{:S(2)}) copy-start(f32[1,16]{1,0:T(1,128)} %param.31) | copy-start | bytes 196
  251.5 164.7 %copy-start.18 = (f32[1,16,601]{2,1,0:T(8,128)S(1)}, f32[1,16,601]{2,1,0:T(8,128)}, u32[]{:S(2)}) copy-start(f32[1,16,601]{2,1,0:T(8,128)} %param.22) | copy-start | bytes 115396
  251.5 164.6 %copy-start.24 = (f32[1,16,601]{2,1,0:T(8,128)S(1)}, f32[1,16,601]{2,1,0:T(8,128)}, u32[]{:S(2)}) copy-start(f32[1,16,601]{2,1,0:T(8,128)} %param.28) | copy-start | bytes 115396
  251.5 164.6 %copy-start.25 = (f32[1,16,601]{2,1,0:T(8,128)S(1)}, f32[1,16,601]{2,1,0:T(8,128)}, u32[]{:S(2)}) copy-start(f32[1,16,601]{2,1,0:T(8,128)} %param.29) | copy-start | bytes 115396
  251.5 243.1 %copy-start.13 = (f32[3,3,16,128]{3,2,1,0:T(8,128)S(1)}, f32[3,3,16,128]{3,2,1,0:T(8,128)}, u32[]{:S(2)}) copy-start(f32[3,3,16,128]{3,2,1,0:T(8,128)} %param.21) | copy-start | bytes 221188
  251.5 243.1 %copy-start.20 = (f32[3,3,16,128]{3,2,1,0:T(8,128)S(1)}, f32[3,3,16,128]{3,2,1,0:T(8,128)}, u32[]{:S(2)}) copy-start(f32[3,3,16,128]{3,2,1,0:T(8,128)} %param.26) | copy-start | bytes 221188
  251.5 243.1 %copy-start.21 = (f32[3,3,16,128]{3,2,1,0:T(8,128)S(1)}, f32[3,3,16,128]{3,2,1,0:T(8,128)}, u32[]{:S(2)}) copy-start(f32[3,3,16,128]{3,2,1,0:T(8,128)} %param.27) | copy-start | bytes 221188
  251.5 321.5 %copy-start.14 = (f32[3,3,16,128]{3,2,1,0:T(8,128)S(1)}, f32[3,3,16,128]{3,2,1,0:T(8,128)}, u32[]{:S(2)}) copy-start(f32[3,3,16,128]{3,2,1,0:T(8,128)} %param.20) | copy-start | bytes 221188
  251.6 321.5 %copy-start.22 = (f32[3,3,16,128]{3,2,1,0:T(8,128)S(1)}, f32[3,3,16,128]{3,2,1,0:T(8,128)}, u32[]{:S(2)}) copy-start(f32[3,3,16,128]{3,2,1,0:T(8,128)} %param.24) | copy-start | bytes 221188
  251.6 321.4 %copy-start.23 = (f32[3,3,16,128]{3,2,1,0:T(8,128)S(1)}, f32[3,3,16,128]{3,2,1,0:T(8,128)}, u32[]{:S(2)}) copy-start(f32[3,3,16,128]{3,2,1,0:T(8,128)} %param.25) | copy-start | bytes 221188
  255.7 160.4 %reduce-scatter.20.cloned.1.call-start = ((), (), s32[]{:S(2)}) async-start(), calls=%async_computation.14 | async-start | bytes 696320 | tf_op jit(solution)/shard_map/reduce_scatter | solution.py:219
  256.5 238.2 %reduce-scatter.16.cloned.1.call-start = ((), (), s32[]{:S(2)}) async-start(), calls=%async_computation.12 | async-start | bytes 1253376 | tf_op jit(solution)/shard_map/reduce_scatter | solution.py:218
  257.2 315.8 %reduce-scatter.12.cloned.1.call-start = ((), (), s32[]{:S(2)}) async-start(), calls=%async_computation.10 | async-start | bytes 1253376 | tf_op jit(solution)/shard_map/reduce_scatter | solution.py:217
  340.0 234.7 %copy-start.27 = (f32[1,16]{1,0:T(1,128)}, f32[1,16]{1,0:T(1,128)S(1)}, u32[]{:S(2)}) copy-start(f32[1,16]{1,0:T(1,128)S(1)} %copy.107) | copy-start | bytes 196
Sparse Core Ops, SparseCore 0:
  56.7 4.7 all-gather.3
  98.7 6.9 all-gather.5
  217.8 6.4 reduce-scatter.17
  237.7 7.6 reduce-scatter.13
  249.0 9.7 reduce-scatter.9
  260.9 78.2 reduce-scatter.21
  342.0 74.0 reduce-scatter.19
  419.0 75.6 reduce-scatter.15
  497.5 75.4 reduce-scatter.11
where the time goes:
time: 582 us; the launch traced here: 581 us
  waiting for transfers between devices  313 us (54%)
  blocking collectives  172 us (30%)
  matrix products  33.7 us (6%)
  other arithmetic  24.3 us (4%)
  between operations  19.6 us (3%)
  local copies, waits for them, and re-layouts  18.2 us (3%)
    unnamed x10, waiting for transfers between devices  81.8 us
    reduce_scatter x1, waiting for transfers between devices, local(): lax.psum_scatter(second_grad, 'dp', scatter_dimension=2, tiled=True)  77.1 us
    reduce_scatter x1, waiting for transfers between devices, local(): lax.psum_scatter(first_grad, 'dp', scatter_dimension=2, tiled=True)  76.8 us
    reduce_scatter x1, waiting for transfers between devices, local(): lax.psum_scatter(head_grad, 'dp', scatter_dimension=1, tiled=True)  75.6 us
    all_gather x1, blocking collectives, local(): lax.all_gather(kernel_first.astype(jnp.bfloat16), 'dp', axis=2, tiled=True)  48.3 us
    unnamed x2, blocking collectives  41.3 us
    all_gather x1, blocking collectives, local(): lax.all_gather(kernel_second.astype(jnp.bfloat16), 'dp', axis=2, tiled=True)  41 us
    all_gather x1, blocking collectives, local(): lax.all_gather(head_weight.astype(jnp.bfloat16), 'dp', axis=1, tiled=True)  37.2 us
  transfers between devices with their start and end apart: 9, of which 5 were waited for; matrix products, arithmetic and copies ran while one was open for 8% of the time, Pallas kernels for 0%

commit v1 on v0

--- a/solution.py
+++ b/solution.py
@@ -1,6 +1,10 @@
+import functools
+
 import jax
 import jax.numpy as jnp
 from jax import lax
+from jax.experimental import pallas as pl
+from jax.experimental.pallas import tpu as pltpu
 from jax.sharding import PartitionSpec as P
 
 CHANNELS = 256
@@ -97,7 +101,7 @@
     return (param_new, mean_new, square_new)
 
 
-def local(
+def local_plain(
     hidden_state,
     actions,
     value_target,
@@ -251,6 +255,538 @@
     )
 
 
+MESH_ID = pl.DeviceIdType.MESH
+LINK = jnp.bfloat16
+
+
+def places(nz):
+    me = lax.axis_index("dp")
+    core = lax.axis_index("mp")
+    z, y, x = me // 4, (me // 2) % 2, me % 2
+    return z, y, x, core
+
+
+def index_of(z, y, x):
+    return z * 4 + y * 2 + x
+
+
+def greet(nz):
+    z, y, x, core = places(nz)
+    barrier = pltpu.get_barrier_semaphore()
+    partners = [(index_of((z + d) % nz, y, x), core) for d in range(1, nz)]
+    partners += [
+        (index_of(z, 1 - y, x), core),
+        (index_of(z, y, 1 - x), core),
+        (index_of(z, y, x), 1 - core),
+    ]
+    for partner in partners:
+        pl.semaphore_signal(barrier, inc=1, device_id=partner, device_id_type=MESH_ID)
+    pl.semaphore_wait(barrier, len(partners))
+
+
+def gather_kernel(nz, ins, outs, local_sem, send_sem, recv_sem):
+    z, y, x, core = places(nz)
+    greet(nz)
+    x_first = (True, False, False)
+
+    def spot(which, d, near, far):
+        zz = (z + d) % nz
+        flip_x, flip_y = (near, far) if x_first[which] else (far, near)
+        yy = 1 - y if flip_y else y
+        xx = 1 - x if flip_x else x
+        return zz, yy, xx
+
+    def copy(which, slot, block, target, own):
+        zz, yy, xx = block
+        dst = outs[which].at[core, :, zz, yy, xx]
+        return pltpu.make_async_remote_copy(
+            src_ref=ins[which] if own else dst,
+            dst_ref=dst,
+            send_sem=send_sem.at[which, slot],
+            recv_sem=recv_sem.at[which, slot],
+            device_id=target,
+            device_id_type=MESH_ID,
+        )
+
+    def arrival(which, slot, block, from_core):
+        zz, yy, xx = block
+        dst = outs[which].at[from_core, :, zz, yy, xx]
+        pltpu.make_async_remote_copy(
+            src_ref=dst,
+            dst_ref=dst,
+            send_sem=send_sem.at[which, slot],
+            recv_sem=recv_sem.at[which, slot],
+            device_id=(index_of(z, y, x), 1 - core),
+            device_id_type=MESH_ID,
+        ).wait_recv()
+
+    started = []
+
+    def send(which, slot, block, target, own=False):
+        handle = copy(which, slot, block, target, own)
+        handle.start()
+        started.append(handle)
+
+    def target_of(which, near, far):
+        flip_x, flip_y = (near, far) if x_first[which] else (far, near)
+        return (index_of(z, 1 - y if flip_y else y, 1 - x if flip_x else x), core)
+
+    partner = (index_of(z, y, x), 1 - core)
+    arrays = range(len(outs))
+    keep = []
+    for d in range(1, nz):
+        for which in arrays:
+            send(which, d, (z, y, x), (index_of((z + d) % nz, y, x), core), True)
+    for which in arrays:
+        send(which, nz, (z, y, x), target_of(which, True, False), True)
+        send(which, 2 * nz, (z, y, x), target_of(which, False, True), True)
+        send(which, 4 * nz, (z, y, x), partner, True)
+        mine = pltpu.make_async_copy(
+            ins[which], outs[which].at[core, :, z, y, x], local_sem.at[which]
+        )
+        mine.start()
+        keep.append(mine)
+    for d in range(1, nz):
+        back = nz - d
+        for which in arrays:
+            block = spot(which, back, False, False)
+            arrival(which, d, block, core)
+            send(which, nz + back, block, target_of(which, True, False))
+            send(which, 2 * nz + back, block, target_of(which, False, True))
+            send(which, 4 * nz + back, block, partner)
+    order = [0] + [nz - d for d in range(1, nz)]
+    for d in order:
+        for which in arrays:
+            block = spot(which, d, True, False)
+            arrival(which, nz + d, block, core)
+            send(which, 3 * nz + d, block, target_of(which, False, True))
+            send(which, 5 * nz + d, block, partner)
+    for near in range(2):
+        for d in order:
+            for which in arrays:
+                block = spot(which, d, near == 1, True)
+                arrival(which, (2 + near) * nz + d, block, core)
+                send(which, (6 + near) * nz + d, block, partner)
+    for far in range(2):
+        for near in range(2):
+            for d in order:
+                for which in arrays:
+                    block = spot(which, d, near == 1, far == 1)
+                    arrival(which, (4 + 2 * far + near) * nz + d, block, 1 - core)
+    for handle in keep:
+        handle.wait()
+    for handle in started:
+        handle.wait_send()
+
+
+def gather_call(nz, blocks):
+    count = len(blocks)
+
+    def body(*refs):
+        gather_kernel(nz, refs[:count], refs[count : 2 * count], *refs[2 * count :])
+
+    vmem = pl.BlockSpec(memory_space=pltpu.VMEM)
+    return pl.pallas_call(
+        body,
+        out_shape=[
+            jax.ShapeDtypeStruct((2, b.shape[0], nz, 2, 2) + b.shape[1:], b.dtype) for b in blocks
+        ],
+        in_specs=[vmem] * count,
+        out_specs=[vmem] * count,
+        scratch_shapes=[
+            pltpu.SemaphoreType.DMA((count,)),
+            pltpu.SemaphoreType.DMA((count, 8 * nz)),
+            pltpu.SemaphoreType.DMA((count, 8 * nz)),
+        ],
+        compiler_params=pltpu.CompilerParams(collective_id=0, has_side_effects=True),
+        name="weights_gather",
+    )(*blocks)
+
+
+def reduce_kernel(nz, parts, outs, bufs, send_sem, recv_sem):
+    z, y, x, core = places(nz)
+    greet(nz)
+    y_first = (True, False, True)
+    arrays = range(len(outs))
+    order = list(range(1, nz)) + [0]
+    started = []
+
+    def send(which, stage, d, src, dst, target):
+        handle = pltpu.make_async_remote_copy(
+            src_ref=src,
+            dst_ref=dst,
+            send_sem=send_sem.at[which, stage, d],
+            recv_sem=recv_sem.at[which, stage, d],
+            device_id=target,
+            device_id_type=MESH_ID,
+        )
+        handle.start()
+        started.append(handle)
+        return handle
+
+    handles = {}
+    for d in order:
+        for which in arrays:
+            handles[which, 0, d] = send(
+                which,
+                0,
+                d,
+                parts[which].at[1 - core, :, (z + d) % nz],
+                bufs[which][0].at[d],
+                (index_of(z, y, x), 1 - core),
+            )
+
+    def first(which, d):
+        got, one = bufs[which][0], bufs[which][1]
+        handles[which, 0, d].wait_recv()
+        for row in range(2):
+            one[d, :, row] = (
+                parts[which][core, :, (z + d) % nz, row].astype(jnp.float32)
+                + got[d, :, row].astype(jnp.float32)
+            ).astype(LINK)
+        if y_first[which]:
+            src, target = one.at[d, :, 1 - y], (index_of(z, 1 - y, x), core)
+        else:
+            src, target = one.at[d, :, :, 1 - x], (index_of(z, y, 1 - x), core)
+        handles[which, 1, d] = send(which, 1, d, src, bufs[which][2].at[d], target)
+
+    def second(which, d):
+        one, got, two = bufs[which][1], bufs[which][2], bufs[which][3]
+        handles[which, 1, d].wait_recv()
+        own = one[d, :, y] if y_first[which] else one[d, :, :, x]
+        two[d] = (own.astype(jnp.float32) + got[d].astype(jnp.float32)).astype(LINK)
+        if y_first[which]:
+            src, target = two.at[d, :, 1 - x], (index_of(z, y, 1 - x), core)
+        else:
+            src, target = two.at[d, :, 1 - y], (index_of(z, 1 - y, x), core)
+        handles[which, 2, d] = send(which, 2, d, src, bufs[which][4].at[d], target)
+
+    def third(which, d):
+        two, got, three = bufs[which][3], bufs[which][4], bufs[which][5]
+        handles[which, 2, d].wait_recv()
+        own = two[d, :, x] if y_first[which] else two[d, :, y]
+        total = own.astype(jnp.float32) + got[d].astype(jnp.float32)
+        if d == 0:
+            outs[which][...] = total
+        else:
+            three[d] = total.astype(LINK)
+            handles[which, 3, d] = send(
+                which,
+                3,
+                d,
+                three.at[d],
+                bufs[which][6].at[d],
+                (index_of((z + d) % nz, y, x), core),
+            )
+
+    for step in range(nz + 2):
+        for stage, act in enumerate((first, second, third)):
+            if 0 <= step - stage < nz:
+                for which in arrays:
+                    act(which, order[step - stage])
+    for which in arrays:
+        total = outs[which][...]
+        for d in range(1, nz):
+            handles[which, 3, d].wait_recv()
+            total = total + bufs[which][6][d].astype(jnp.float32)
+        outs[which][...] = total
+    for handle in started:
+        handle.wait_send()
+
+
+def reduce_call(nz, parts):
+    count = len(parts)
+
+    def body(*refs):
+        held = refs[2 * count :]
+        bufs = [held[7 * i : 7 * i + 7] for i in range(count)]
+        reduce_kernel(nz, refs[:count], refs[count : 2 * count], bufs, *held[7 * count :])
+
+    vmem = pl.BlockSpec(memory_space=pltpu.VMEM)
+    scratch, shapes = [], []
+    for p in parts:
+        taps, rows, lanes = p.shape[1], p.shape[5], p.shape[6]
+        four, two, one = (nz, taps, 2, 2, rows, lanes), (nz, taps, 2, rows, lanes), (nz, taps, rows, lanes)
+        scratch += [pltpu.VMEM(s, LINK) for s in (four, four, two, two, one, one, one)]
+        shapes.append(jax.ShapeDtypeStruct((taps, rows, lanes), jnp.float32))
+    scratch += [pltpu.SemaphoreType.DMA((count, 4, nz)), pltpu.SemaphoreType.DMA((count, 4, nz))]
+    return pl.pallas_call(
+        body,
+        out_shape=shapes,
+        in_specs=[vmem] * count,
+        out_specs=[vmem] * count,
+        scratch_shapes=scratch,
+        compiler_params=pltpu.CompilerParams(
+            collective_id=1, has_side_effects=True, vmem_limit_bytes=60 * 2**20
+        ),
+        name="gradients_reduce",
+    )(*parts)
+
+
+def step_kernel(
+    total, board, pitch, buckets, acts, values, rewards, field, first, second, heads,
+    first_out, second_out, head_out,
+    in_wide, hid_wide, pre_held, sum_held, state_held, carry_held, first_acc, second_acc,
+    head_left, head_right, small,
+):
+    count, unroll = acts.shape
+    rows = board * pitch
+    channels = field.shape[2]
+    lanes = heads.shape[3]
+    cells = board * board
+    scale = (9.0 * channels) ** (-0.5)
+    f32 = jnp.float32
+
+    def grid_iota(axis):
+        return lax.broadcasted_iota(jnp.int32, (board, pitch, channels), axis)
+
+    def inside():
+        return (grid_iota(1) < board).reshape(rows, channels)
+
+    def spread(value):
+        return jnp.concatenate(
+            [pltpu.roll(value, 1, 0), value, pltpu.roll(value, rows - 1, 0)], axis=1
+        ).astype(jnp.bfloat16)
+
+    def down(value):
+        return jnp.concatenate([jnp.zeros((pitch, channels), f32), value[: rows - pitch]], axis=0)
+
+    def up(value):
+        return jnp.concatenate([value[pitch:], jnp.zeros((pitch, channels), f32)], axis=0)
+
+    def tap(ref, offset):
+        return jnp.concatenate([ref[0, offset], ref[1, offset]], axis=1)
+
+    def conv(wide, ref, flip, turned):
+        rows_out = None
+        for a in (1, 0, 2):
+            part = None
+            for b in range(3):
+                offset = 8 - (a * 3 + b) if flip else a * 3 + b
+                piece = lax.dot_general(
+                    wide[:, b * channels : (b + 1) * channels],
+                    tap(ref, offset),
+                    (((1,), (1 if turned else 0,)), ((), ())),
+                    preferred_element_type=f32,
+                )
+                part = piece if part is None else part + piece
+            if a == 0:
+                part = down(part)
+            elif a == 2:
+                part = up(part)
+            rows_out = part if rows_out is None else rows_out + part
+        return jnp.where(inside(), rows_out, 0.0)
+
+    def outer(left, right):
+        return lax.dot_general(
+            left, right, (((0,), (0,)), ((), ())), preferred_element_type=f32
+        )
+
+    lane = lax.broadcasted_iota(jnp.int32, (8, lanes), 1)
+    row_small = lax.broadcasted_iota(jnp.int32, (8, lanes), 0)
+    row_chan = lax.broadcasted_iota(jnp.int32, (8, channels), 0)
+    mark = jnp.where(lane == buckets, 1.0, 0.0).astype(jnp.bfloat16)
+
+    def head_of(h):
+        return heads[h, 0]
+
+    def lane_dot(left, right):
+        return lax.dot_general(
+            left, right, (((1,), (1,)), ((), ())), preferred_element_type=f32
+        )
+
+    embed = [lane_dot(mark, head_of(h))[0:1] for h in range(2)]
+
+    first_acc[...] = jnp.zeros_like(first_acc)
+    second_acc[...] = jnp.zeros_like(second_acc)
+
+    for n in range(count):
+        head_left[...] = jnp.zeros_like(head_left)
+        head_right[...] = jnp.zeros_like(head_right)
+        state_held[...] = field[n].astype(f32)
+
+        def forward(k, _):
+            move = acts[n, k]
+            spot = jnp.where(
+                grid_iota(1) < board, grid_iota(0) * board + grid_iota(1), -1
+            ).reshape(rows, channels)
+            passed = jnp.where(move == cells, 1.0, 0.0)
+            mixed = state_held[...] + jnp.where(spot == move, embed[0], 0.0)
+            mixed = mixed + jnp.where(spot >= 0, passed * embed[1], 0.0)
+            sum_held[k] = mixed
+            in_wide[k] = spread(mixed)
+            pre = scale * conv(in_wide[k], first, False, False)
+            pre_held[k] = pre
+            hid_wide[k] = spread((pre * jax.nn.sigmoid(pre)).astype(jnp.bfloat16).astype(f32))
+            summed = sum_held[k] + scale * conv(hid_wide[k], second, False, True)
+            sum_held[k] = summed
+            factor = lax.rsqrt(jnp.sum(summed * summed) / (cells * channels) + eps_norm)
+            state = summed * factor
+            state_held[...] = state
+            pooled = (jnp.sum(state, axis=0, keepdims=True) / cells).astype(jnp.bfloat16)
+            pooled8 = jnp.broadcast_to(pooled.astype(f32), (8, channels)).astype(jnp.bfloat16)
+            pooled_grad = jnp.zeros((8, channels), f32)
+            for h, targets in ((0, values), (1, rewards)):
+                raw = head_scale * jnp.dot(pooled8, head_of(h), preferred_element_type=f32)
+                squashed = jnp.tanh(raw / soft_cap)
+                raised = jnp.where(lane < buckets, jnp.exp(soft_cap * squashed), 0.0)
+                chances = raised / jnp.sum(raised, axis=1, keepdims=True)
+                picked = jnp.where(lane == targets[n, k], 1.0, 0.0)
+                grad = (chances - picked) * (1.0 - squashed * squashed) / total
+                grad = jnp.where(lane < buckets, grad, 0.0)
+                grad16 = grad.astype(jnp.bfloat16)
+                pooled_grad = pooled_grad + lane_dot(grad16, head_of(h))
+                head_right[h] = jnp.where(row_small == k, grad16.astype(f32), head_right[h])
+                head_left[h] = jnp.where(row_chan == k, pooled8.astype(f32), head_left[h])
+            small[k, 0] = head_scale * pooled_grad / cells
+            small[k, 1] = jnp.full((8, channels), factor, f32)
+            return 0
+
+        lax.fori_loop(0, unroll, forward, 0)
+        carry_held[...] = jnp.zeros_like(carry_held)
+
+        def backward(step, sums):
+            k = unroll - 1 - step
+            move = acts[n, k]
+            factor = small[k, 1][0:1]
+            summed = sum_held[k]
+            state_grad = jnp.where(inside(), carry_held[...] + small[k, 0][0:1], 0.0)
+            dots = jnp.sum(state_grad * summed) / (cells * channels)
+            summed_grad = factor * state_grad - factor * factor * factor * summed * dots
+            state_held[...] = summed_grad
+            branch = summed_grad.astype(jnp.bfloat16).astype(f32)
+            hidden_grad = scale * conv(spread(branch), second, True, False)
+            pre = pre_held[k]
+            sig = jax.nn.sigmoid(pre)
+            inner = (hidden_grad * (sig * (1.0 + pre * (1.0 - sig)))).astype(jnp.bfloat16).astype(f32)
+            carry = state_held[...] + scale * conv(spread(inner), first, True, True)
+            carry_held[...] = carry
+            for a in range(3):
+                move_rows = (up, lambda v: v, down)[a]
+                inner_a = move_rows(inner).astype(jnp.bfloat16)
+                branch_a = move_rows(branch).astype(jnp.bfloat16)
+                for b in range(3):
+                    cut = slice(b * channels, (b + 1) * channels)
+                    first_acc[a * 3 + b] += outer(in_wide[k, :, cut], inner_a)
+                    second_acc[a * 3 + b] += outer(branch_a, hid_wide[k, :, cut])
+            spot = jnp.where(
+                grid_iota(1) < board, grid_iota(0) * board + grid_iota(1), -1
+            ).reshape(rows, channels)
+            at_cell = jnp.sum(jnp.where(spot == move, carry, 0.0), axis=0, keepdims=True)
+            at_pass = jnp.sum(carry, axis=0, keepdims=True) * jnp.where(move == cells, 1.0, 0.0)
+            return sums[0] + at_cell, sums[1] + at_pass
+
+        none = jnp.zeros((1, channels), f32)
+        sums = lax.fori_loop(0, unroll, backward, (none, none))
+        for h in range(2):
+            left = jnp.where(row_chan == unroll, sums[h] / head_scale, head_left[h])
+            right = jnp.where((row_small == unroll) & (lane == buckets), 1.0, head_right[h])
+            grad = head_scale * outer(left.astype(jnp.bfloat16), right.astype(jnp.bfloat16))
+            if n == 0:
+                head_out[h, 0] = grad.astype(LINK)
+            else:
+                head_out[h, 0] = (head_out[h, 0].astype(f32) + grad).astype(LINK)
+    half = channels // 2
+    for offset in range(9):
+        for core in range(2):
+            cut = slice(core * half, (core + 1) * half)
+            first_out[core, offset] = (scale * first_acc[offset, :, cut]).astype(LINK)
+            second_out[core, offset] = (scale * second_acc[offset, :, cut]).astype(LINK)
+
+
+def step_call(total, board, buckets, acts, values, rewards, field, first, second, heads):
+    pitch = -(-(board + 1) // 8) * 8
+    count, unroll = acts.shape
+    channels = field.shape[3]
+    lanes = heads.shape[3]
+    rows = board * pitch
+    field = jnp.pad(field, ((0, 0), (0, 0), (0, pitch - board), (0, 0))).reshape(count, rows, channels)
+    vmem = pl.BlockSpec(memory_space=pltpu.VMEM)
+    smem = pl.BlockSpec(memory_space=pltpu.SMEM)
+    f32 = jnp.float32
+    return pl.pallas_call(
+        functools.partial(step_kernel, total, board, pitch, buckets),
+        out_shape=[jax.ShapeDtypeStruct(a.shape, LINK) for a in (first, second, heads)],
+        in_specs=[smem] * 3 + [vmem] * 4,
+        out_specs=[vmem] * 3,
+        scratch_shapes=[
+            pltpu.VMEM((unroll, rows, 3 * channels), jnp.bfloat16),
+            pltpu.VMEM((unroll, rows, 3 * channels), jnp.bfloat16),
+            pltpu.VMEM((unroll, rows, channels), f32),
+            pltpu.VMEM((unroll, rows, channels), f32),
+            pltpu.VMEM((rows, channels), f32),
+            pltpu.VMEM((rows, channels), f32),
+            pltpu.VMEM((9, channels, channels), f32),
+            pltpu.VMEM((9, channels, channels), f32),
+            pltpu.VMEM((2, 8, channels), f32),
+            pltpu.VMEM((2, 8, lanes), f32),
+            pltpu.VMEM((unroll, 2, 8, channels), f32),
+        ],
+        compiler_params=pltpu.CompilerParams(vmem_limit_bytes=60 * 2**20),
+        name="learner_step",
+    )(acts, values, rewards, field, first, second, heads)
+
+
+def local(*args):
+    (hidden_state, actions, value_target, reward_target, kernel_first, kernel_second, head_weight,
+     action_embed, first_mean, first_square, second_mean, second_square, head_mean, head_square,
+     embed_mean, embed_square) = args
+    span, cores = lax.axis_size("dp"), lax.axis_size("mp")
+    slab = kernel_first.shape[2]
+    if cores != 2 or span % 4 or slab % 16 or actions.shape[1] > 7:
+        return local_plain(*args)
+    nz = span // 4
+    buckets = head_weight.shape[2]
+    lanes = -(-(buckets + 1) // 128) * 128
+    half = kernel_first.shape[3]
+    channels = span * slab
+
+    def pack(weights, column):
+        joined = jnp.concatenate([weights, column[:, :, None]], axis=2).astype(LINK)
+        return jnp.pad(joined, ((0, 0), (0, 0), (0, lanes - buckets - 1)))
+
+    blocks = (
+        kernel_first.astype(LINK).reshape(9, slab, half),
+        kernel_second.astype(LINK).reshape(9, slab, half),
+        pack(head_weight, action_embed),
+    )
+    used = gather_call(nz, blocks)
+    count = hidden_state.shape[0] // cores
+    begin = lax.axis_index("mp") * count
+
+    def own(array):
+        return lax.dynamic_slice_in_dim(array, begin, count, 0)
+
+    flat = [u.reshape(2, u.shape[1], channels, u.shape[6]) for u in used]
+    parts = step_call(
+        hidden_state.shape[0] * span, hidden_state.shape[1], buckets,
+        own(actions), own(value_target), own(reward_target), own(hidden_state), *flat,
+    )
+    sums = reduce_call(nz, [p.reshape(u.shape) for p, u in zip(parts, used)])
+    first_grad = sums[0].reshape(kernel_first.shape)
+    second_grad = sums[1].reshape(kernel_second.shape)
+    head_grad = sums[2][:, :, :buckets]
+    embed_grad = sums[2][:, :, buckets]
+    first_new, first_mean_new, first_square_new = adam_update(
+        kernel_first, first_grad, first_mean, first_square
+    )
+    second_new, second_mean_new, second_square_new = adam_update(
+        kernel_second, second_grad, second_mean, second_square
+    )
+    head_new, head_mean_new, head_square_new = adam_update(
+        head_weight, head_grad, head_mean, head_square
+    )
+    embed_new, embed_mean_new, embed_square_new = adam_update(
+        action_embed, embed_grad, embed_mean, embed_square
+    )
+    return (
+        first_new, second_new, head_new, embed_new,
+        first_mean_new, first_square_new, second_mean_new, second_square_new,
+        head_mean_new, head_square_new, embed_mean_new, embed_square_new,
+        first_grad, second_grad, head_grad, embed_grad,
+    )
+
+
 def solution(mesh):
     placed = (
         P("dp", None, None, None),

time: 582 us -> 85.8 us (0.15)
  waiting for transfers between devices: 313 us -> 0 us
  blocking collectives: 172 us -> 0 us
  Pallas kernels: 0 us -> 68.1 us
  matrix products: 33.7 us -> 0 us
  between operations: 19.6 us -> 0.84 us
  other arithmetic: 24.3 us -> 10.3 us
  local copies, waits for them, and re-layouts: 18.2 us -> 5.95 us
    reduce_scatter x6 -> x0, waiting for transfers between devices: 231 us -> none  [the longest x1 77.1 us: local(): lax.psum_scatter(second_grad, 'dp', scatter_dimension=2, tiled=True)]
    all_gather x5 -> x0, blocking collectives: 131 us -> none  [the longest x1 48.3 us: local(): lax.all_gather(kernel_first.astype(jnp.bfloat16), 'dp', axis=2, tiled=True)]
    unnamed x10 -> x0, waiting for transfers between devices: 81.8 us -> none
    pallas_call x0 -> x3, Pallas kernels: none -> 68.1 us  [the longest x1 26.8 us: gather_call(): pl.pallas_call(body, out_shape=[jax.ShapeDtypeStruct((2, b.shape[0], nz,...]
    unnamed x2 -> x0, blocking collectives: 41.3 us -> none
    dot_general x44 -> x0, matrix products: 21.2 us -> none  [the longest x18 14.7 us: tap_products(): lax.dot_general(flat_grad, window, (((0,), (0,)), ((), ())), preferred_el...]
    conv_general_dilated x8 -> x0, matrix products: 12.5 us -> none  [conv_apply(): lax.conv_general_dilated(field, kernel, (1, 1), 'SAME', dimension_numbers...]
    unnamed x86 -> x35, local copies, waits for them, and re-layouts: 7.99 us -> 1.39 us
  transfers between devices with their start and end apart: 9 -> 0, of which waited for: 5 -> 0; matrix products, arithmetic and copies ran while one was open for 8% -> 0% of each run, Pallas kernels for 0% -> 0%
where the time goes in v1:
time: 85.8 us; the launch traced here: 85.2 us
  Pallas kernels  68.1 us (79%)
  other arithmetic  10.3 us (12%)
  local copies, waits for them, and re-layouts  5.95 us (7%)
    pallas_call x1, Pallas kernels, gather_call(): pl.pallas_call(body, out_shape=[jax.ShapeDtypeStruct((2, b.shape[0], nz,...  26.8 us
    pallas_call x1, Pallas kernels, reduce_call(): pl.pallas_call(body, out_shape=shapes, in_specs=[vmem] * count, out_specs...  25.1 us
    pallas_call x1, Pallas kernels, step_call(): pl.pallas_call(functools.partial(step_kernel, total, board, pitch, bucket...  16.2 us
    sub x4, other arithmetic, adam_update(): param_new = param - step_size * mean_new / (jnp.sqrt(square_new) + eps_adam)  5.15 us
    dynamic_slice x3, local copies, waits for them, and re-layouts, own(): return lax.dynamic_slice_in_dim(array, begin, count, 0)  2.84 us

profile of v1, /device:TPU:0, one launch (start us, length us, event | category | flops | bytes accessed | tf_op | source)
XLA Modules:
  0.0 85.2 jit_solution(90542365886258653)
XLA Ops:
  0.6 0.0 copy-start
  0.7 1.2 %constant_dynamic-slice_fusion.3.acts = s32[1,2]{1,0:T(1,128)} fusion(s32[2,2]{1,0:T(2,128)} %param.17, s32[]{:T(128)S(6)} %select_n.2), kind=kLoop, calls=%fused_computation.20 | loop fusion | bytes 20 | tf_op jit(solution)/shard_map/dynamic_slice | solution.py:758
  1.9 0.7 convert_bitcast_fusion
  2.6 1.2 %constant_dynamic-slice_fusion.1 = (s32[1,2]{1,0:T(1,128)}, s32[1,2]{1,0:T(1,128)}) fusion(s32[2,2]{1,0:T(2,128)} %param.19, s32[]{:T(128)S(6)} %select_n.2, s32[2,2]{1,0:T(2,128)} %param.18), kind=kLoop, calls=%fused_computation.18 | loop fusion | bytes 36 | tf_op jit(solution)/shard_map/dynamic_slice | solution.py:758
  3.8 0.1 copy.34
  3.9 0.8 convert.7
  4.7 0.7 fusion.5.refs_2_
  5.3 1.5 %convert_element_type.19 = bf16[3,3,16,128]{3,2,1,0:T(8,128)(2,1)} convert(f32[3,3,16,128]{3,2,1,0:T(8,128)} %param.20) | non-fusion elementwise | flops 18432 | bytes 110592 | tf_op jit(solution)/shard_map/convert_element_type | solution.py:749
  6.9 1.5 %convert_element_type.20 = bf16[3,3,16,128]{3,2,1,0:T(8,128)(2,1)} convert(f32[3,3,16,128]{3,2,1,0:T(8,128)} %param.21) | non-fusion elementwise | flops 18432 | bytes 110592 | tf_op jit(solution)/shard_map/convert_element_type | solution.py:750
  8.4 0.0 copy-done
  8.4 0.4 constant_dynamic-slice_fusion
  8.8 0.7 pad.8
  9.5 26.8 %weights_gather.1 = (bf16[2,9,4,2,2,16,128]{6,5,4,3,2,1,0:T(8,128)(2,1)}, bf16[2,9,4,2,2,16,128]{6,5,4,3,2,1,0:T(8,128)(2,1)}, bf16[2,1,4,2,2,16,640]{6,5,4,3,2,1,0:T(8,128)(2,1)}) custom-call(bf16[9,16,128]{2,1,0:T(8,128)(2,1)} %bitcast.26, bf16[9,16,128]{2,1,0:T(8,128)(2,1)} %bitcast.27, bf16[1,16,640]{2,1,0:T(8,128)(2,1)} %fusion.5.refs_2_), custom_call_target="tpu_custom_call" | custom-call | tf_op jit(solution)/shard_map/weights_gather/pallas_call | solution.py:389
  36.3 16.2 %learner_step.1 = (bf16[2,9,256,128]{3,2,1,0:T(8,128)(2,1)}, bf16[2,9,256,128]{3,2,1,0:T(8,128)(2,1)}, bf16[2,1,256,640]{3,2,1,0:T(8,128)(2,1)}) custom-call(s32[1,2]{1,0:T(1,128)} %constant_dynamic-slice_fusion.3.acts, s32[1,2]{1,0:T(1,128)} %get-tuple-element.48.values, s32[1,2]{1,0:T(1,128)} %get-tuple-element.47.rewards, bf16[1,456,256]{2,1,0:T(8,128)(2,1)} %bitcast.19, ...), custom_call_target="tpu_custom_call" | custom-call | tf_op jit(solution)/shard_map/learner_step/pallas_call | solution.py:707
  52.5 0.0 copy-start.15
  52.6 0.0 copy-start.5
  52.6 0.0 copy-start.10
  52.6 0.0 copy-start.11
  52.6 0.0 copy-start.1
  52.6 0.0 copy-start.6
  52.6 0.0 copy-start.7
  52.6 0.0 copy-start.2
  52.6 0.0 copy-start.8
  52.7 0.0 copy-start.9
  52.7 25.1 %gradients_reduce.1 = (f32[9,16,128]{2,1,0:T(8,128)}, f32[9,16,128]{2,1,0:T(8,128)}, f32[1,16,640]{2,1,0:T(8,128)}) custom-call(bf16[2,9,4,2,2,16,128]{6,5,4,3,2,1,0:T(8,128)(2,1)} %bitcast.17, bf16[2,9,4,2,2,16,128]{6,5,4,3,2,1,0:T(8,128)(2,1)} %bitcast.18, bf16[2,1,4,2,2,16,640]{6,5,4,3,2,1,0:T(8,128)(2,1)} %bitcast.21), custom_call_target="tpu_custom_call" | custom-call | tf_op jit(solution)/shard_map/gradients_reduce/pallas_call | solution.py:513
  77.8 0.0 copy-start.4
  77.8 0.0 copy-start.3
  77.8 0.9 %slice_reduce_fusion = f32[16]{0:T(128)S(1)} fusion(f32[1,16,640]{2,1,0:T(8,128)} %get-tuple-element.33), kind=kLoop, calls=%fused_computation.16 | loop fusion | bytes 128 | tf_op jit(solution)/shard_map/slice | solution.py:769
  78.7 0.0 copy-done.13
  78.7 0.0 copy-done.14
  78.7 0.0 copy-done.15
  78.7 0.5 divide_subtract_fusion.3
  79.3 0.0 copy-done.5
  79.3 0.0 copy-done.10
  79.3 0.0 copy-done.11
  79.3 1.4 %divide_subtract_fusion.2 = (f32[1,16,601]{2,1,0:T(8,128)}, f32[1,16,601]{2,1,0:T(8,128)}, f32[1,16,601]{2,1,0:T(8,128)}, f32[1,16,601]{2,1,0:T(8,128)}) fusion(f32[1,16,601]{2,1,0:T(8,128)S(1)} %copy-done.5, f32[1,16,601]{2,1,0:T(8,128)S(1)} %copy-done.10, f32[1,16,601]{2,1,0:T(8,128)S(1)} %copy-done.11, f32[1,16,640]{2,1,0:T(8,128)} %get-tuple-element.33), kind=kLoop, calls=%fused_computation.13 | loop fusion | flops 105776 | bytes 307712 | tf_op jit(solution)/shard_map/sub | solution.py:100
  80.7 0.0 copy-done.1
  80.7 0.0 copy-done.6
  80.7 0.0 copy-done.7
  80.7 1.6 %divide_subtract_fusion.1 = (f32[3,3,16,128]{3,2,1,0:T(8,128)}, f32[3,3,16,128]{3,2,1,0:T(8,128)}, f32[3,3,16,128]{3,2,1,0:T(8,128)}) fusion(f32[3,3,16,128]{3,2,1,0:T(8,128)S(1)} %copy-done.1, f32[3,3,16,128]{3,2,1,0:T(8,128)} %bitcast.24, f32[3,3,16,128]{3,2,1,0:T(8,128)S(1)} %copy-done.6, f32[3,3,16,128]{3,2,1,0:T(8,128)S(1)} %copy-done.7), kind=kLoop, calls=%fused_computation.6 | loop fusion | flops 202752 | bytes 516096 | tf_op jit(solution)/shard_map/sub | solution.py:100
  82.3 0.0 copy-done.2
  82.3 0.0 copy-done.8
  82.3 0.0 copy-done.9
  82.3 1.6 %divide_subtract_fusion = (f32[3,3,16,128]{3,2,1,0:T(8,128)}, f32[3,3,16,128]{3,2,1,0:T(8,128)}, f32[3,3,16,128]{3,2,1,0:T(8,128)}) fusion(f32[3,3,16,128]{3,2,1,0:T(8,128)S(1)} %copy-done.2, f32[3,3,16,128]{3,2,1,0:T(8,128)} %bitcast.22, f32[3,3,16,128]{3,2,1,0:T(8,128)S(1)} %copy-done.8, f32[3,3,16,128]{3,2,1,0:T(8,128)S(1)} %copy-done.9), kind=kLoop, calls=%fused_computation.4 | loop fusion | flops 202752 | bytes 516096 | tf_op jit(solution)/shard_map/sub | solution.py:100
  83.9 0.0 copy-done.4
  83.9 0.6 copy.38
  84.6 0.6 copy.39
  85.2 0.0 copy-done.12
  (5 shorter events, 0.0 us)
Async XLA Ops:
  0.6 7.7 %copy-start = (bf16[2,19,19,256]{3,0,2,1:T(2,128)(2,1)S(1)}, bf16[2,19,19,256]{3,0,2,1:T(2,128)(2,1)}, u32[]{:S(2)}) copy-start(bf16[2,19,19,256]{3,0,2,1:T(2,128)(2,1)} %param.16) | copy-start | bytes 1108996
  52.5 26.2 %copy-start.13 = (f32[1,16]{1,0:T(1,128)S(1)}, f32[1,16]{1,0:T(1,128)}, u32[]{:S(2)}) copy-start(f32[1,16]{1,0:T(1,128)} %param.23) | copy-start | bytes 196
  52.5 26.2 %copy-start.14 = (f32[1,16]{1,0:T(1,128)S(1)}, f32[1,16]{1,0:T(1,128)}, u32[]{:S(2)}) copy-start(f32[1,16]{1,0:T(1,128)} %param.30) | copy-start | bytes 196
  52.5 26.2 %copy-start.15 = (f32[1,16]{1,0:T(1,128)S(1)}, f32[1,16]{1,0:T(1,128)}, u32[]{:S(2)}) copy-start(f32[1,16]{1,0:T(1,128)} %param.31) | copy-start | bytes 196
  52.6 26.7 %copy-start.5 = (f32[1,16,601]{2,1,0:T(8,128)S(1)}, f32[1,16,601]{2,1,0:T(8,128)}, u32[]{:S(2)}) copy-start(f32[1,16,601]{2,1,0:T(8,128)} %param.22) | copy-start | bytes 115396
  52.6 26.7 %copy-start.10 = (f32[1,16,601]{2,1,0:T(8,128)S(1)}, f32[1,16,601]{2,1,0:T(8,128)}, u32[]{:S(2)}) copy-start(f32[1,16,601]{2,1,0:T(8,128)} %param.28) | copy-start | bytes 115396
  52.6 26.7 %copy-start.11 = (f32[1,16,601]{2,1,0:T(8,128)S(1)}, f32[1,16,601]{2,1,0:T(8,128)}, u32[]{:S(2)}) copy-start(f32[1,16,601]{2,1,0:T(8,128)} %param.29) | copy-start | bytes 115396
  52.6 28.1 %copy-start.1 = (f32[3,3,16,128]{3,2,1,0:T(8,128)S(1)}, f32[3,3,16,128]{3,2,1,0:T(8,128)}, u32[]{:S(2)}) copy-start(f32[3,3,16,128]{3,2,1,0:T(8,128)} %param.20) | copy-start | bytes 221188
  52.6 28.1 %copy-start.6 = (f32[3,3,16,128]{3,2,1,0:T(8,128)S(1)}, f32[3,3,16,128]{3,2,1,0:T(8,128)}, u32[]{:S(2)}) copy-start(f32[3,3,16,128]{3,2,1,0:T(8,128)} %param.24) | copy-start | bytes 221188
  52.6 28.1 %copy-start.7 = (f32[3,3,16,128]{3,2,1,0:T(8,128)S(1)}, f32[3,3,16,128]{3,2,1,0:T(8,128)}, u32[]{:S(2)}) copy-start(f32[3,3,16,128]{3,2,1,0:T(8,128)} %param.25) | copy-start | bytes 221188
  52.6 29.7 %copy-start.2 = (f32[3,3,16,128]{3,2,1,0:T(8,128)S(1)}, f32[3,3,16,128]{3,2,1,0:T(8,128)}, u32[]{:S(2)}) copy-start(f32[3,3,16,128]{3,2,1,0:T(8,128)} %param.21) | copy-start | bytes 221188
  52.6 29.7 %copy-start.8 = (f32[3,3,16,128]{3,2,1,0:T(8,128)S(1)}, f32[3,3,16,128]{3,2,1,0:T(8,128)}, u32[]{:S(2)}) copy-start(f32[3,3,16,128]{3,2,1,0:T(8,128)} %param.26) | copy-start | bytes 221188
  52.7 29.7 %copy-start.9 = (f32[3,3,16,128]{3,2,1,0:T(8,128)S(1)}, f32[3,3,16,128]{3,2,1,0:T(8,128)}, u32[]{:S(2)}) copy-start(f32[3,3,16,128]{3,2,1,0:T(8,128)} %param.27) | copy-start | bytes 221188
  77.8 6.2 %copy-start.4 = (f32[9,16,128]{2,1,0:T(8,128)S(1)}, f32[9,16,128]{2,1,0:T(8,128)}, u32[]{:S(2)}) copy-start(f32[9,16,128]{2,1,0:T(8,128)} %get-tuple-element.31) | copy-start | bytes 221188
  77.8 6.8 %copy-start.3 = (f32[9,16,128]{2,1,0:T(8,128)S(1)}, f32[9,16,128]{2,1,0:T(8,128)}, u32[]{:S(2)}) copy-start(f32[9,16,128]{2,1,0:T(8,128)} %get-tuple-element.32) | copy-start | bytes 221188
  78.7 6.5 %copy-start.12 = (f32[16]{0:T(128)}, f32[16]{0:T(128)S(1)}, u32[]{:S(2)}) copy-start(f32[16]{0:T(128)S(1)} %slice_reduce_fusion) | copy-start | bytes 196

commit v2 on v1

--- a/solution.py
+++ b/solution.py
@@ -284,8 +284,23 @@
     pl.semaphore_wait(barrier, len(partners))
 
 
-def gather_kernel(nz, ins, outs, local_sem, send_sem, recv_sem):
+def gather_kernel(nz, raw, outs, ins, local_sem, send_sem, recv_sem):
     z, y, x, core = places(nz)
+    ins[0][...] = raw[0][...].astype(LINK)
+    ins[1][...] = raw[1][...].astype(LINK)
+    _, slab, buckets = raw[2].shape
+    lanes = ins[2].shape[2]
+    eye = lax.broadcasted_iota(jnp.int32, (slab, slab), 0) == lax.broadcasted_iota(
+        jnp.int32, (slab, slab), 1
+    )
+    column = jnp.sum(jnp.where(eye, raw[3][...], 0.0), axis=1, keepdims=True)
+    aligned = buckets // 128 * 128
+    tail = jnp.concatenate(
+        [raw[2][0, :, aligned:], jnp.zeros((slab, lanes - buckets), jnp.float32)], axis=1
+    )
+    at = lax.broadcasted_iota(jnp.int32, tail.shape, 1) + aligned
+    ins[2][0, :, :aligned] = raw[2][0, :, :aligned].astype(LINK)
+    ins[2][0, :, aligned:] = jnp.where(at == buckets, column, tail).astype(LINK)
     greet(nz)
     x_first = (True, False, False)
 
@@ -298,7 +313,7 @@
 
     def copy(which, slot, block, target, own):
         zz, yy, xx = block
-        dst = outs[which].at[core, :, zz, yy, xx]
+        dst = outs[which].at[core, zz, yy, xx]
         return pltpu.make_async_remote_copy(
             src_ref=ins[which] if own else dst,
             dst_ref=dst,
@@ -310,7 +325,7 @@
 
     def arrival(which, slot, block, from_core):
         zz, yy, xx = block
-        dst = outs[which].at[from_core, :, zz, yy, xx]
+        dst = outs[which].at[from_core, zz, yy, xx]
         pltpu.make_async_remote_copy(
             src_ref=dst,
             dst_ref=dst,
@@ -342,7 +357,7 @@
         send(which, 2 * nz, (z, y, x), target_of(which, False, True), True)
         send(which, 4 * nz, (z, y, x), partner, True)
         mine = pltpu.make_async_copy(
-            ins[which], outs[which].at[core, :, z, y, x], local_sem.at[which]
+            ins[which], outs[which].at[core, z, y, x], local_sem.at[which]
         )
         mine.start()
         keep.append(mine)
@@ -379,28 +394,30 @@
         handle.wait_send()
 
 
-def gather_call(nz, blocks):
-    count = len(blocks)
+def gather_call(nz, lanes, first, second, head, embed):
+    shapes = [first.shape, second.shape, head.shape[:2] + (lanes,)]
+    count = len(shapes)
 
     def body(*refs):
-        gather_kernel(nz, refs[:count], refs[count : 2 * count], *refs[2 * count :])
+        gather_kernel(nz, refs[:4], refs[4:7], refs[7:10], *refs[10:])
 
     vmem = pl.BlockSpec(memory_space=pltpu.VMEM)
     return pl.pallas_call(
         body,
         out_shape=[
-            jax.ShapeDtypeStruct((2, b.shape[0], nz, 2, 2) + b.shape[1:], b.dtype) for b in blocks
+            jax.ShapeDtypeStruct((2, nz, 2, 2) + s, LINK) for s in shapes
         ],
-        in_specs=[vmem] * count,
+        in_specs=[vmem] * 4,
         out_specs=[vmem] * count,
-        scratch_shapes=[
+        scratch_shapes=[pltpu.VMEM(s, LINK) for s in shapes]
+        + [
             pltpu.SemaphoreType.DMA((count,)),
             pltpu.SemaphoreType.DMA((count, 8 * nz)),
             pltpu.SemaphoreType.DMA((count, 8 * nz)),
         ],
         compiler_params=pltpu.CompilerParams(collective_id=0, has_side_effects=True),
         name="weights_gather",
-    )(*blocks)
+    )(first, second, head, embed)
 
 
 def reduce_kernel(nz, parts, outs, bufs, send_sem, recv_sem):
@@ -431,7 +448,7 @@
                 which,
                 0,
                 d,
-                parts[which].at[1 - core, :, (z + d) % nz],
+                parts[which].at[1 - core, (z + d) % nz],
                 bufs[which][0].at[d],
                 (index_of(z, y, x), 1 - core),
             )
@@ -440,31 +457,31 @@
         got, one = bufs[which][0], bufs[which][1]
         handles[which, 0, d].wait_recv()
         for row in range(2):
-            one[d, :, row] = (
-                parts[which][core, :, (z + d) % nz, row].astype(jnp.float32)
-                + got[d, :, row].astype(jnp.float32)
+            one[d, row] = (
+                parts[which][core, (z + d) % nz, row].astype(jnp.float32)
+                + got[d, row].astype(jnp.float32)
             ).astype(LINK)
         if y_first[which]:
-            src, target = one.at[d, :, 1 - y], (index_of(z, 1 - y, x), core)
+            src, target = one.at[d, 1 - y], (index_of(z, 1 - y, x), core)
         else:
-            src, target = one.at[d, :, :, 1 - x], (index_of(z, y, 1 - x), core)
+            src, target = one.at[d, :, 1 - x], (index_of(z, y, 1 - x), core)
         handles[which, 1, d] = send(which, 1, d, src, bufs[which][2].at[d], target)
 
     def second(which, d):
         one, got, two = bufs[which][1], bufs[which][2], bufs[which][3]
         handles[which, 1, d].wait_recv()
-        own = one[d, :, y] if y_first[which] else one[d, :, :, x]
+        own = one[d, y] if y_first[which] else one[d, :, x]
         two[d] = (own.astype(jnp.float32) + got[d].astype(jnp.float32)).astype(LINK)
         if y_first[which]:
-            src, target = two.at[d, :, 1 - x], (index_of(z, y, 1 - x), core)
+            src, target = two.at[d, 1 - x], (index_of(z, y, 1 - x), core)
         else:
-            src, target = two.at[d, :, 1 - y], (index_of(z, 1 - y, x), core)
+            src, target = two.at[d, 1 - y], (index_of(z, 1 - y, x), core)
         handles[which, 2, d] = send(which, 2, d, src, bufs[which][4].at[d], target)
 
     def third(which, d):
         two, got, three = bufs[which][3], bufs[which][4], bufs[which][5]
         handles[which, 2, d].wait_recv()
-        own = two[d, :, x] if y_first[which] else two[d, :, y]
+        own = two[d, x] if y_first[which] else two[d, y]
         total = own.astype(jnp.float32) + got[d].astype(jnp.float32)
         if d == 0:
             outs[which][...] = total
@@ -505,8 +522,9 @@
     vmem = pl.BlockSpec(memory_space=pltpu.VMEM)
     scratch, shapes = [], []
     for p in parts:
-        taps, rows, lanes = p.shape[1], p.shape[5], p.shape[6]
-        four, two, one = (nz, taps, 2, 2, rows, lanes), (nz, taps, 2, rows, lanes), (nz, taps, rows, lanes)
+        taps, rows, lanes = p.shape[4:]
+        one = (nz, taps, rows, lanes)
+        two, four = (nz, 2) + one[1:], (nz, 2, 2) + one[1:]
         scratch += [pltpu.VMEM(s, LINK) for s in (four, four, two, two, one, one, one)]
         shapes.append(jax.ShapeDtypeStruct((taps, rows, lanes), jnp.float32))
     scratch += [pltpu.SemaphoreType.DMA((count, 4, nz)), pltpu.SemaphoreType.DMA((count, 4, nz))]
@@ -529,10 +547,13 @@
     in_wide, hid_wide, pre_held, sum_held, state_held, carry_held, first_acc, second_acc,
     head_left, head_right, small,
 ):
-    count, unroll = acts.shape
+    unroll = acts.shape[1]
+    count = field.shape[0]
+    begin = lax.axis_index("mp") * count
     rows = board * pitch
     channels = field.shape[2]
-    lanes = heads.shape[3]
+    lanes = heads.shape[4]
+    span, slab = first.shape[1], first.shape[3]
     cells = board * board
     scale = (9.0 * channels) ** (-0.5)
     f32 = jnp.float32
@@ -555,7 +576,9 @@
         return jnp.concatenate([value[pitch:], jnp.zeros((pitch, channels), f32)], axis=0)
 
     def tap(ref, offset):
-        return jnp.concatenate([ref[0, offset], ref[1, offset]], axis=1)
+        return jnp.concatenate(
+            [ref[core, :, offset].reshape(channels, channels // 2) for core in range(2)], axis=1
+        )
 
     def conv(wide, ref, flip, turned):
         rows_out = None
@@ -588,7 +611,7 @@
     mark = jnp.where(lane == buckets, 1.0, 0.0).astype(jnp.bfloat16)
 
     def head_of(h):
-        return heads[h, 0]
+        return heads[h].reshape(channels, lanes)
 
     def lane_dot(left, right):
         return lax.dot_general(
@@ -606,7 +629,7 @@
         state_held[...] = field[n].astype(f32)
 
         def forward(k, _):
-            move = acts[n, k]
+            move = acts[begin + n, k]
             spot = jnp.where(
                 grid_iota(1) < board, grid_iota(0) * board + grid_iota(1), -1
             ).reshape(rows, channels)
@@ -631,7 +654,7 @@
                 squashed = jnp.tanh(raw / soft_cap)
                 raised = jnp.where(lane < buckets, jnp.exp(soft_cap * squashed), 0.0)
                 chances = raised / jnp.sum(raised, axis=1, keepdims=True)
-                picked = jnp.where(lane == targets[n, k], 1.0, 0.0)
+                picked = jnp.where(lane == targets[begin + n, k], 1.0, 0.0)
                 grad = (chances - picked) * (1.0 - squashed * squashed) / total
                 grad = jnp.where(lane < buckets, grad, 0.0)
                 grad16 = grad.astype(jnp.bfloat16)
@@ -647,7 +670,7 @@
 
         def backward(step, sums):
             k = unroll - 1 - step
-            move = acts[n, k]
+            move = acts[begin + n, k]
             factor = small[k, 1][0:1]
             summed = sum_held[k]
             state_grad = jnp.where(inside(), carry_held[...] + small[k, 0][0:1], 0.0)
@@ -682,23 +705,27 @@
             left = jnp.where(row_chan == unroll, sums[h] / head_scale, head_left[h])
             right = jnp.where((row_small == unroll) & (lane == buckets), 1.0, head_right[h])
             grad = head_scale * outer(left.astype(jnp.bfloat16), right.astype(jnp.bfloat16))
-            if n == 0:
-                head_out[h, 0] = grad.astype(LINK)
-            else:
-                head_out[h, 0] = (head_out[h, 0].astype(f32) + grad).astype(LINK)
+            grad = grad.reshape(span, 1, slab, lanes)
+            if n > 0:
+                grad = grad + head_out[h].astype(f32)
+            head_out[h] = grad.astype(LINK)
     half = channels // 2
     for offset in range(9):
         for core in range(2):
             cut = slice(core * half, (core + 1) * half)
-            first_out[core, offset] = (scale * first_acc[offset, :, cut]).astype(LINK)
-            second_out[core, offset] = (scale * second_acc[offset, :, cut]).astype(LINK)
+            first_out[core, :, offset] = (
+                (scale * first_acc[offset, :, cut]).astype(LINK).reshape(span, slab, half)
+            )
+            second_out[core, :, offset] = (
+                (scale * second_acc[offset, :, cut]).astype(LINK).reshape(span, slab, half)
+            )
 
 
 def step_call(total, board, buckets, acts, values, rewards, field, first, second, heads):
     pitch = -(-(board + 1) // 8) * 8
-    count, unroll = acts.shape
-    channels = field.shape[3]
-    lanes = heads.shape[3]
+    unroll = acts.shape[1]
+    count, channels = field.shape[0], field.shape[3]
+    lanes = heads.shape[4]
     rows = board * pitch
     field = jnp.pad(field, ((0, 0), (0, 0), (0, pitch - board), (0, 0))).reshape(count, rows, channels)
     vmem = pl.BlockSpec(memory_space=pltpu.VMEM)
@@ -739,52 +766,75 @@
     buckets = head_weight.shape[2]
     lanes = -(-(buckets + 1) // 128) * 128
     half = kernel_first.shape[3]
-    channels = span * slab
-
-    def pack(weights, column):
-        joined = jnp.concatenate([weights, column[:, :, None]], axis=2).astype(LINK)
-        return jnp.pad(joined, ((0, 0), (0, 0), (0, lanes - buckets - 1)))
-
-    blocks = (
-        kernel_first.astype(LINK).reshape(9, slab, half),
-        kernel_second.astype(LINK).reshape(9, slab, half),
-        pack(head_weight, action_embed),
-    )
-    used = gather_call(nz, blocks)
+
+    used = gather_call(
+        nz,
+        lanes,
+        kernel_first.reshape(9, slab, half),
+        kernel_second.reshape(9, slab, half),
+        head_weight,
+        action_embed,
+    )
     count = hidden_state.shape[0] // cores
     begin = lax.axis_index("mp") * count
 
-    def own(array):
-        return lax.dynamic_slice_in_dim(array, begin, count, 0)
-
-    flat = [u.reshape(2, u.shape[1], channels, u.shape[6]) for u in used]
+    states = lax.dynamic_slice_in_dim(hidden_state, begin, count, 0)
+    flat = [u.reshape((2, span) + u.shape[4:]) for u in used]
     parts = step_call(
         hidden_state.shape[0] * span, hidden_state.shape[1], buckets,
-        own(actions), own(value_target), own(reward_target), own(hidden_state), *flat,
+        actions, value_target, reward_target, states, *flat,
     )
     sums = reduce_call(nz, [p.reshape(u.shape) for p, u in zip(parts, used)])
-    first_grad = sums[0].reshape(kernel_first.shape)
-    second_grad = sums[1].reshape(kernel_second.shape)
-    head_grad = sums[2][:, :, :buckets]
-    embed_grad = sums[2][:, :, buckets]
-    first_new, first_mean_new, first_square_new = adam_update(
-        kernel_first, first_grad, first_mean, first_square
-    )
-    second_new, second_mean_new, second_square_new = adam_update(
-        kernel_second, second_grad, second_mean, second_square
-    )
-    head_new, head_mean_new, head_square_new = adam_update(
-        head_weight, head_grad, head_mean, head_square
-    )
-    embed_new, embed_mean_new, embed_square_new = adam_update(
-        action_embed, embed_grad, embed_mean, embed_square
-    )
+    def flatten(array):
+        return array.reshape(9, slab, half)
+
+    outs = adam_call(
+        buckets,
+        *sums,
+        *[flatten(a) for a in (kernel_first, first_mean, first_square)],
+        *[flatten(a) for a in (kernel_second, second_mean, second_square)],
+        head_weight, head_mean, head_square,
+        action_embed, embed_mean, embed_square,
+    )
+    shaped = [o.reshape(kernel_first.shape) if o.ndim == 3 and o.shape[0] == 9 else o for o in outs]
+    first, second, head, embed = (shaped[4 * i : 4 * i + 4] for i in range(4))
     return (
-        first_new, second_new, head_new, embed_new,
-        first_mean_new, first_square_new, second_mean_new, second_square_new,
-        head_mean_new, head_square_new, embed_mean_new, embed_square_new,
-        first_grad, second_grad, head_grad, embed_grad,
-    )
+        first[0], second[0], head[0], embed[0],
+        first[1], first[2], second[1], second[2],
+        head[1], head[2], embed[1], embed[2],
+        first[3], second[3], head[3], embed[3],
+    )
+
+
+def adam_kernel(buckets, *refs):
+    sums, old, new = refs[:3], refs[3:15], refs[15:]
+    slab = sums[2].shape[1]
+    eye = lax.broadcasted_iota(jnp.int32, (slab, slab), 0) == lax.broadcasted_iota(
+        jnp.int32, (slab, slab), 1
+    )
+    embed_grad = jnp.sum(
+        jnp.where(eye, sums[2][0, :, buckets : buckets + 1], 0.0), axis=0, keepdims=True
+    )
+    grads = (sums[0][...], sums[1][...], sums[2][:, :, :buckets], embed_grad)
+    for i, grad in enumerate(grads):
+        param, mean, square = (old[3 * i + j][...] for j in range(3))
+        made = adam_update(param, grad, mean, square) + (grad,)
+        for j in range(4):
+            new[4 * i + j][...] = made[j]
+
+
+def adam_call(buckets, *arrays):
+    vmem = pl.BlockSpec(memory_space=pltpu.VMEM)
+    shapes = []
+    for i in range(4):
+        shapes += [jax.ShapeDtypeStruct(arrays[3 + 3 * i].shape, jnp.float32)] * 4
+    return pl.pallas_call(
+        functools.partial(adam_kernel, buckets),
+        out_shape=shapes,
+        in_specs=[vmem] * len(arrays),
+        out_specs=[vmem] * len(shapes),
+        name="adam",
+    )(*arrays)
 
 
 def solution(mesh):

time: 85.8 us -> 73.4 us (0.86)
  other arithmetic: 10.3 us -> 0 us
  local copies, waits for them, and re-layouts: 5.95 us -> 2.11 us
  Pallas kernels: 68.1 us -> 70.3 us
    sub x4 -> x0, other arithmetic: 5.15 us -> none  [adam_update(): param_new = param - step_size * mean_new / (jnp.sqrt(square_new) + eps_adam)]
    convert_element_type x2 -> x0, other arithmetic: 3.01 us -> none  [the longest x1 1.51 us: local(): kernel_first.astype(LINK).reshape(9, slab, half)]
    dynamic_slice x3 -> x1, local copies, waits for them, and re-layouts: 2.84 us -> 0.39 us  [local(): states = lax.dynamic_slice_in_dim(hidden_state, begin, count, 0)]
    pallas_call x1 -> x2, Pallas kernels: 26.8 us -> 29.2 us  [the longest x1 27 us: gather_call(): pl.pallas_call(body, out_shape=[jax.ShapeDtypeStruct((2, nz, 2, 2) + s, L...]
    concatenate x2 -> x0, other arithmetic: 1.34 us -> none  [pack(): joined = jnp.concatenate([weights, column[:, :, None]], axis=2).astype(LINK)]
    slice x1 -> x0, local copies, waits for them, and re-layouts: 0.91 us -> none  [local(): embed_grad = sums[2][:, :, buckets]]
where the time goes in v2:
time: 73.4 us; the launch traced here: 73.1 us
  Pallas kernels  70.3 us (96%)
  local copies, waits for them, and re-layouts  2.11 us (3%)
    pallas_call x1, Pallas kernels, gather_call(): pl.pallas_call(body, out_shape=[jax.ShapeDtypeStruct((2, nz, 2, 2) + s, L...  27 us
    pallas_call x1, Pallas kernels, reduce_call(): pl.pallas_call(body, out_shape=shapes, in_specs=[vmem] * count, out_specs...  24.9 us
    pallas_call x1, Pallas kernels, step_call(): pl.pallas_call(functools.partial(step_kernel, total, board, pitch, bucket...  16.3 us
    pallas_call x1, Pallas kernels, adam_call(): pl.pallas_call(functools.partial(adam_kernel, buckets), out_shape=shapes,...  2.19 us

profile of v2, /device:TPU:0, one launch (start us, length us, event | category | flops | bytes accessed | tf_op | source)
XLA Modules:
  0.0 73.1 jit_solution(922127955266177935)
XLA Ops:
  0.6 0.0 copy-start
  0.7 1.0 %copy-done = bf16[2,19,19,256]{3,0,2,1:T(2,128)(2,1)S(1)} copy-done((bf16[2,19,19,256]{3,0,2,1:T(2,128)(2,1)S(1)}, bf16[2,19,19,256]{3,0,2,1:T(2,128)(2,1)}, u32[]{:S(2)}) %copy-start) | copy-done | bytes 369688
  1.6 0.4 constant_dynamic-slice_fusion
  2.1 0.7 pad.4
  2.8 27.0 %weights_gather.1 = (bf16[2,4,2,2,9,16,128]{6,5,4,3,2,1,0:T(8,128)(2,1)}, bf16[2,4,2,2,9,16,128]{6,5,4,3,2,1,0:T(8,128)(2,1)}, bf16[2,4,2,2,1,16,640]{6,5,4,3,2,1,0:T(8,128)(2,1)}) custom-call(f32[9,16,128]{2,1,0:T(8,128)} %bitcast.28, f32[9,16,128]{2,1,0:T(8,128)} %bitcast.30, f32[1,16,601]{2,1,0:T(8,128)} %refs_9_.1, f32[1,16]{1,0:T(1,128)} %refs_12_.1), custom_call_target="tpu_custom_call" | custom-call | tf_op jit(solution)/shard_map/weights_gather/pallas_call | solution.py:405
  29.8 16.3 %learner_step.1 = (bf16[2,16,9,16,128]{4,3,2,1,0:T(8,128)(2,1)}, bf16[2,16,9,16,128]{4,3,2,1,0:T(8,128)(2,1)}, bf16[2,16,1,16,640]{4,3,2,1,0:T(8,128)(2,1)}) custom-call(s32[2,2]{1,0:T(2,128)} %acts.1, s32[2,2]{1,0:T(2,128)} %values.1, s32[2,2]{1,0:T(2,128)} %rewards.1, bf16[1,456,256]{2,1,0:T(8,128)(2,1)} %bitcast.25, ...), custom_call_target="tpu_custom_call" | custom-call | tf_op jit(solution)/shard_map/learner_step/pallas_call | solution.py:734
  46.0 24.9 %gradients_reduce.1 = (f32[9,16,128]{2,1,0:T(8,128)}, f32[9,16,128]{2,1,0:T(8,128)}, f32[1,16,640]{2,1,0:T(8,128)}) custom-call(bf16[2,4,2,2,9,16,128]{6,5,4,3,2,1,0:T(8,128)(2,1)} %bitcast.21, bf16[2,4,2,2,9,16,128]{6,5,4,3,2,1,0:T(8,128)(2,1)} %bitcast.22, bf16[2,4,2,2,1,16,640]{6,5,4,3,2,1,0:T(8,128)(2,1)} %bitcast.26), custom_call_target="tpu_custom_call" | custom-call | tf_op jit(solution)/shard_map/gradients_reduce/pallas_call | solution.py:531
  70.9 2.2 %adam.1 = (f32[9,16,128]{2,1,0:T(8,128)}, f32[9,16,128]{2,1,0:T(8,128)}, f32[9,16,128]{2,1,0:T(8,128)}, f32[9,16,128]{2,1,0:T(8,128)}, f32[9,16,128]{2,1,0:T(8,1...) custom-call(f32[9,16,128]{2,1,0:T(8,128)} %get-tuple-element.47.refs, ...), custom_call_target="tpu_custom_call" | custom-call | tf_op jit(solution)/shard_map/adam/pallas_call | solution.py:831
  (1 shorter events, 0.0 us)
Async XLA Ops:
  0.6 1.0 %copy-start = (bf16[2,19,19,256]{3,0,2,1:T(2,128)(2,1)S(1)}, bf16[2,19,19,256]{3,0,2,1:T(2,128)(2,1)}, u32[]{:S(2)}) copy-start(bf16[2,19,19,256]{3,0,2,1:T(2,128)(2,1)} %param.16) | copy-start | bytes 1108996

commit v3 on v2

--- a/solution.py
+++ b/solution.py
@@ -361,7 +361,9 @@
         )
         mine.start()
         keep.append(mine)
-    for d in range(1, nz):
+    order = [0] + [nz - d for d in range(1, nz)]
+
+    def from_z(d):
         back = nz - d
         for which in arrays:
             block = spot(which, back, False, False)
@@ -369,19 +371,31 @@
             send(which, nz + back, block, target_of(which, True, False))
             send(which, 2 * nz + back, block, target_of(which, False, True))
             send(which, 4 * nz + back, block, partner)
-    order = [0] + [nz - d for d in range(1, nz)]
-    for d in order:
+
+    def from_near(d):
         for which in arrays:
             block = spot(which, d, True, False)
             arrival(which, nz + d, block, core)
             send(which, 3 * nz + d, block, target_of(which, False, True))
             send(which, 5 * nz + d, block, partner)
-    for near in range(2):
-        for d in order:
-            for which in arrays:
-                block = spot(which, d, near == 1, True)
-                arrival(which, (2 + near) * nz + d, block, core)
-                send(which, (6 + near) * nz + d, block, partner)
+
+    def from_far(near, d):
+        for which in arrays:
+            block = spot(which, d, near == 1, True)
+            arrival(which, (2 + near) * nz + d, block, core)
+            send(which, (6 + near) * nz + d, block, partner)
+
+    from_near(0)
+    for d in range(1, nz):
+        from_z(d)
+        if d > 1:
+            from_near(order[d - 1])
+        from_far(0, order[d - 1])
+    if nz > 1:
+        from_near(order[nz - 1])
+    from_far(0, order[nz - 1])
+    for d in order:
+        from_far(1, d)
     for far in range(2):
         for near in range(2):
             for d in order:
@@ -778,6 +792,7 @@
     count = hidden_state.shape[0] // cores
     begin = lax.axis_index("mp") * count
 
+    used, hidden_state = lax.optimization_barrier((tuple(used), hidden_state))
     states = lax.dynamic_slice_in_dim(hidden_state, begin, count, 0)
     flat = [u.reshape((2, span) + u.shape[4:]) for u in used]
     parts = step_call(

time: 73.4 us -> 73.5 us (level)
    optimization_barrier x0 -> x1, local copies, waits for them, and re-layouts: none -> 1.05 us  [local(): used, hidden_state = lax.optimization_barrier((tuple(used), hidden_state))]
    unnamed x3 -> x0, local copies, waits for them, and re-layouts: 1.02 us -> none
where the time goes in v3:
time: 73.5 us; the launch traced here: 73.2 us
  Pallas kernels  70.8 us (96%)
  local copies, waits for them, and re-layouts  1.79 us (2%)
    pallas_call x1, Pallas kernels, gather_call(): pl.pallas_call(body, out_shape=[jax.ShapeDtypeStruct((2, nz, 2, 2) + s, L...  27.6 us
    pallas_call x1, Pallas kernels, reduce_call(): pl.pallas_call(body, out_shape=shapes, in_specs=[vmem] * count, out_specs...  24.7 us
    pallas_call x1, Pallas kernels, step_call(): pl.pallas_call(functools.partial(step_kernel, total, board, pitch, bucket...  16.2 us
    pallas_call x1, Pallas kernels, adam_call(): pl.pallas_call(functools.partial(adam_kernel, buckets), out_shape=shapes,...  2.19 us

profile of v3, /device:TPU:0, one launch (start us, length us, event | category | flops | bytes accessed | tf_op | source)
XLA Modules:
  0.0 73.2 jit_solution(6692406116093099792)
XLA Ops:
  0.6 27.6 %weights_gather.1 = (bf16[2,4,2,2,9,16,128]{6,5,4,3,2,1,0:T(8,128)(2,1)}, bf16[2,4,2,2,9,16,128]{6,5,4,3,2,1,0:T(8,128)(2,1)}, bf16[2,4,2,2,1,16,640]{6,5,4,3,2,1,0:T(8,128)(2,1)}) custom-call(f32[9,16,128]{2,1,0:T(8,128)} %bitcast.28, f32[9,16,128]{2,1,0:T(8,128)} %bitcast.30, f32[1,16,601]{2,1,0:T(8,128)} %refs_9_.1, f32[1,16]{1,0:T(1,128)} %refs_12_.1), custom_call_target="tpu_custom_call" | custom-call | tf_op jit(solution)/shard_map/weights_gather/pallas_call | solution.py:419
  28.3 1.1 %copy.32 = bf16[2,19,19,256]{3,2,1,0:T(8,128)(2,1)S(1)} copy(bf16[2,19,19,256]{3,0,2,1:T(2,128)(2,1)} %param.16) | data formatting | bytes 739328 | tf_op jit(solution)/shard_map/optimization_barrier | solution.py:795
  29.4 0.7 pad.4
  30.1 16.2 %learner_step.1 = (bf16[2,16,9,16,128]{4,3,2,1,0:T(8,128)(2,1)}, bf16[2,16,9,16,128]{4,3,2,1,0:T(8,128)(2,1)}, bf16[2,16,1,16,640]{4,3,2,1,0:T(8,128)(2,1)}) custom-call(s32[2,2]{1,0:T(2,128)} %acts.1, s32[2,2]{1,0:T(2,128)} %values.1, s32[2,2]{1,0:T(2,128)} %rewards.1, bf16[1,456,256]{2,1,0:T(8,128)(2,1)} %bitcast.25, ...), custom_call_target="tpu_custom_call" | custom-call | tf_op jit(solution)/shard_map/learner_step/pallas_call | solution.py:748
  46.3 24.7 %gradients_reduce.1 = (f32[9,16,128]{2,1,0:T(8,128)}, f32[9,16,128]{2,1,0:T(8,128)}, f32[1,16,640]{2,1,0:T(8,128)}) custom-call(bf16[2,4,2,2,9,16,128]{6,5,4,3,2,1,0:T(8,128)(2,1)} %bitcast.23, bf16[2,4,2,2,9,16,128]{6,5,4,3,2,1,0:T(8,128)(2,1)} %bitcast.24, bf16[2,4,2,2,1,16,640]{6,5,4,3,2,1,0:T(8,128)(2,1)} %bitcast.27), custom_call_target="tpu_custom_call" | custom-call | tf_op jit(solution)/shard_map/gradients_reduce/pallas_call | solution.py:545
  71.0 2.2 %adam.1 = (f32[9,16,128]{2,1,0:T(8,128)}, f32[9,16,128]{2,1,0:T(8,128)}, f32[9,16,128]{2,1,0:T(8,128)}, f32[9,16,128]{2,1,0:T(8,128)}, f32[9,16,128]{2,1,0:T(8,1...) custom-call(f32[9,16,128]{2,1,0:T(8,128)} %get-tuple-element.55.refs, ...), custom_call_target="tpu_custom_call" | custom-call | tf_op jit(solution)/shard_map/adam/pallas_call | solution.py:846
  (1 shorter events, 0.0 us)
